TPU v7x, 128 devices: a whole 4x4x4 slice. The times are simulated.
128 devices in a mesh: dp: 8 (over y, core), fsdp: 16 (over z, x).
Axes of the slice: x: 4, y: 4, z: 4, core: 2. Of those that a mesh axis runs over, the one named last changes fastest.
Arguments:
- grad_q: bfloat16 [8, 8192, 8192], P('dp', 'fsdp'), may hold values from -40 to 40, as said below
- grad_k: bfloat16 [8, 8192, 1024], P('dp', 'fsdp'), may hold values from -40 to 40
- grad_v: bfloat16 [8, 8192, 1024], P('dp', 'fsdp'), may hold values from -40 to 40
- proj_q: bfloat16 [8192, 512], P('fsdp'), may hold values from -5 to 5, as said below
- proj_k: bfloat16 [8192, 512], P('fsdp'), may hold values from -5 to 5
- proj_v: bfloat16 [8192, 512], P('fsdp'), may hold values from -5 to 5
- weight_q: bfloat16 [8192, 8192], P('fsdp', 'dp'), may hold values from -4 to 4
- key_weight_matrix: bfloat16 [8192, 1024], P('fsdp', 'dp'), may hold values from -4 to 4
- value_weight_matrix: bfloat16 [8192, 1024], P('fsdp', 'dp'), may hold values from -4 to 4
- comp_q: bfloat16 [8192, 8192], P('fsdp', 'dp'), may hold values from -0.0039978027 to 0.0039978027
- key_compensation: bfloat16 [8192, 1024], P('fsdp', 'dp'), may hold values from -0.0039978027 to 0.0039978027
- value_compensation: bfloat16 [8192, 1024], P('fsdp', 'dp'), may hold values from -0.0039978027 to 0.0039978027
- avg_q: float32 [512, 8192], P('fsdp', 'dp'), may hold values from -1.5 to 1.5
- key_first_moment: float32 [512, 1024], P('fsdp', 'dp'), may hold values from -1.5 to 1.5
- value_first_moment: float32 [512, 1024], P('fsdp', 'dp'), may hold values from -1.5 to 1.5
- sq_q: float32 [512, 8192], P('fsdp', 'dp'), may hold values from 0.001 to 0.1
- key_second_moment: float32 [512, 1024], P('fsdp', 'dp'), may hold values from 0.001 to 0.1
- value_second_moment: float32 [512, 1024], P('fsdp', 'dp'), may hold values from 0.001 to 0.1
Outputs:
- new_weight_q: float32 [8192, 8192], P('fsdp', 'dp')
- new_weight_k: float32 [8192, 1024], P('fsdp', 'dp')
- new_weight_v: float32 [8192, 1024], P('fsdp', 'dp')
- new_avg_q: float32 [512, 8192], P('fsdp', 'dp')
- new_avg_k: float32 [512, 1024], P('fsdp', 'dp')
- new_avg_v: float32 [512, 1024], P('fsdp', 'dp')
- new_sq_q: float32 [512, 8192], P('fsdp', 'dp')
- new_sq_k: float32 [512, 1024], P('fsdp', 'dp')
- new_sq_v: float32 [512, 1024], P('fsdp', 'dp')
Inputs may be any that keep to these rules, and one draw needn't show every extreme that they name: `grad_q`: each partial of the gradients is real-valued and of full rank. `proj_q`: projectors are real-valued and of full rank 512.
All inputs are finite; a program needn't handle non-finite values.
Results may differ from a plain program's by a relative error of at most 0.00044.
Values may be sent and summed in bfloat16 or wider, within the bound.
No kernel may reach another device: no remote copies, remote signals or barrier semaphores. Data moves between devices by JAX's collectives and lax.ppermute only.
A program may use at most 128 MiB of HBM per device.

v0:
```python
import math
import jax
import jax.numpy as jnp
from jax import lax
from jax.sharding import Mesh
from jax.sharding import PartitionSpec as P

QUERY_OUTPUTS = 8192
KEY_VALUE_OUTS = 1024
PROJECT_RANK = 512
STEP = 10
DP = ("dp_0", "dp_1")
FSDP = ("fsdp_0", "fsdp_1")
DP_FSDP = ("dp_0", "dp_1", "fsdp_0", "fsdp_1")


def in_one_piece(arrays, axis, dim, along):
    both = jnp.concatenate(arrays, axis=along)
    whole, at, done = (lax.psum_scatter(both, axis, scatter_dimension=dim, tiled=True), 0, [])
    for a in arrays:
        done.append(lax.slice_in_dim(whole, at, at + a.shape[along], axis=along))
        at += a.shape[along]
    return tuple(done)


def split_up(x, dim, devices):
    lengths = x.shape
    pieces = x.reshape(*lengths[:dim], devices, lengths[dim] // devices, *lengths[dim + 1 :])
    return jnp.moveaxis(pieces, dim, 0)


def sum_at_owner(x, axis, dim):
    pieces = split_up(x, dim, lax.axis_size(axis))
    arrived = lax.all_to_all(pieces, axis, split_axis=0, concat_axis=0, tiled=True)
    return arrived.sum(axis=0)


def sent_together(arrays, axis, dim, along):
    ends, at = ([], 0)
    for a in arrays[:-1]:
        at += a.shape[along]
        ends.append(at)
    both = jnp.concatenate(arrays, axis=along)
    return tuple(jnp.split(sum_at_owner(both, axis, dim), ends, axis=along))


def over_axes(x, axes):
    for axis in axes:
        x = lax.psum(x, axis)
    return x


def from_everyone(x, axis):
    devices = lax.axis_size(axis)
    return lax.all_to_all(jnp.broadcast_to(x[None], (devices, *x.shape)), axis, 0, 0, tiled=True)


def laid_out(pieces, dim):
    pieces = jnp.moveaxis(pieces, 0, dim)
    lengths = pieces.shape
    return pieces.reshape(*lengths[:dim], lengths[dim] * lengths[dim + 1], *lengths[dim + 2 :])


def gather_directly(x, axis, dim):
    pieces = from_everyone(x, axis)
    return laid_out(pieces, dim)


def side_by_side(arrays, axis, dim, along):
    widths = [a.shape[along] for a in arrays]
    both = jnp.concatenate(arrays, axis=along)
    whole = gather_directly(both, axis, dim)
    return tuple(jnp.split(whole, [sum(widths[:k]) for k in range(1, len(widths))], axis=along))


def adam_apply(projected, clip_factor, first_moment, second_moment):
    scaled = clip_factor * projected
    new_avg = 0.9 * first_moment + 0.1 * scaled
    new_sq = 0.95 * second_moment + 0.05 * scaled * scaled
    correct_one = 1.0 - 0.9**STEP
    correct_two = 1.0 - 0.95**STEP
    update = new_avg / correct_one / (jnp.sqrt(new_sq / correct_two) + 1e-08)
    return (new_avg, new_sq, update.astype(jnp.bfloat16))


def shards(
    grad_q,
    grad_k,
    grad_v,
    proj_q,
    proj_k,
    proj_v,
    weight_q,
    key_weight_matrix,
    value_weight_matrix,
    comp_q,
    key_compensation,
    value_compensation,
    avg_q,
    key_first_moment,
    value_first_moment,
    sq_q,
    key_second_moment,
    value_second_moment,
):
    gradients = (grad_q[0], grad_k[0], grad_v[0])
    projectors = (proj_q, proj_k, proj_v)
    weights = (weight_q, key_weight_matrix, value_weight_matrix)
    comps = (comp_q, key_compensation, value_compensation)
    avgs = (avg_q, key_first_moment, value_first_moment)
    squares = (sq_q, key_second_moment, value_second_moment)
    contract_rows = (((0,), (0,)), ((), ()))
    complete = [
        lax.dot_general(projector, gradient, contract_rows, preferred_element_type=jnp.float32)
        for gradient, projector in zip(gradients, projectors)
    ]
    narrow = (
        lax.psum_scatter(complete[0], DP, scatter_dimension=1, tiled=True),
        *in_one_piece((complete[1], complete[2]), DP, 1, 0),
    )
    shares = sent_together((narrow[0], narrow[1], narrow[2]), FSDP, 0, 1)
    local_sum = jnp.zeros((), jnp.float32)
    for member in shares:
        local_sum = local_sum + jnp.sum(member * member)
    square_sum = over_axes(local_sum, DP_FSDP)
    clipping_threshold = math.sqrt(PROJECT_RANK * (QUERY_OUTPUTS + 2 * KEY_VALUE_OUTS))
    clip_factor = jnp.minimum(1.0, clipping_threshold / jnp.sqrt(square_sum + 1e-06))
    new_avgs, new_sqs, updates = ([], [], [])
    for index_mat in range(3):
        new_avg, new_sq, update = adam_apply(
            shares[index_mat], clip_factor, avgs[index_mat], squares[index_mat]
        )
        new_avgs.append(new_avg)
        new_sqs.append(new_sq)
        updates.append(update)
    zero_sums = tuple((jnp.zeros(weight.shape, jnp.float32) for weight in weights))
    pieces = side_by_side((updates[0], updates[1], updates[2]), FSDP, 0, 1)
    results = []
    for total_acc, piece, projector in zip(zero_sums, pieces, projectors):
        results.append(jnp.dot(projector, piece, preferred_element_type=jnp.float32))
    products = (results[0], results[1], results[2])
    new_weights = []
    for index_mat in range(3):
        delta = -0.04 * products[index_mat]
        new_weights.append(
            weights[index_mat].astype(jnp.float32) + (delta + comps[index_mat].astype(jnp.float32))
        )
    return (
        new_weights[0],
        new_weights[1],
        new_weights[2],
        new_avgs[0],
        new_avgs[1],
        new_avgs[2],
        new_sqs[0],
        new_sqs[1],
        new_sqs[2],
    )


def solution(mesh):
    split = Mesh(mesh.devices.reshape(4, 2, 4, 4), ("dp_0", "dp_1", "fsdp_0", "fsdp_1"))
    return jax.shard_map(
        shards,
        mesh=split,
        in_specs=(
            P(DP, FSDP, None),
            P(DP, FSDP, None),
            P(DP, FSDP, None),
            P(FSDP, None),
            P(FSDP, None),
            P(FSDP, None),
            P(FSDP, DP),
            P(FSDP, DP),
            P(FSDP, DP),
            P(FSDP, DP),
            P(FSDP, DP),
            P(FSDP, DP),
            P(FSDP, DP),
            P(FSDP, DP),
            P(FSDP, DP),
            P(FSDP, DP),
            P(FSDP, DP),
            P(FSDP, DP),
        ),
        out_specs=(
            P(FSDP, DP),
            P(FSDP, DP),
            P(FSDP, DP),
            P(FSDP, DP),
            P(FSDP, DP),
            P(FSDP, DP),
            P(FSDP, DP),
            P(FSDP, DP),
            P(FSDP, DP),
        ),
        check_vma=False,
    )
```

profile of v0, /device:TPU:0, one launch (start us, length us, event | category | flops | bytes accessed | tf_op | source)
XLA Modules:
  0.0 268.8 jit_solution(694423666051327244)
XLA Ops:
  7.3 1.1 copy-done
  8.4 1.8 fusion.10
  10.9 2.5 pad_maximum_fusion
  14.4 11.7 %fusion = f32[512,8192]{1,0:T(8,128)} fusion(bf16[512,512]{1,0:T(8,128)(2,1)S(1)} %copy-done.2, bf16[1,512,8192]{2,1,0:T(8,128)(2,1)} %param.18), kind=kOutput, calls=%fused_computation | convolution fusion | flops 4294967296 | bytes 25690112 | tf_op jit(solution)/shard_map/dot_general | solution.py:114
  26.2 27.8 %reduce-scatter.5.cloned.1.call-done = f32[1024,128]{1,0:T(8,128)} async-done(((f32[1024,1024]{1,0:T(8,128)}), f32[1024,128]{1,0:T(8,128)}) %reduce-scatter.5.cloned.1.call-update) | async-done | bytes 524304 | tf_op jit(solution)/shard_map/reduce_scatter | solution.py:19
  54.0 1.1 fusion.22
  55.1 92.1 %reduce-scatter.3.cloned.1.call-done = f32[512,1024]{1,0:T(8,128)} async-done(((f32[512,8192]{1,0:T(8,128)}), f32[512,1024]{1,0:T(8,128)}) %reduce-scatter.3.cloned.1.call-update) | async-done | bytes 2097168 | tf_op jit(solution)/shard_map/reduce_scatter | solution.py:118
  147.2 1.8 pad_maximum_fusion.1
  149.0 40.4 %all_to_all.10 = f32[16,32,1280]{2,1,0:T(8,128)} all-to-all(f32[16,32,1280]{2,1,0:T(8,128)S(1)} %bitcast.33), channel_id=1, replica_groups=mesh['dp_0'=4,'dp_1'=2,'fsdp_0'=4,'fsdp_1'=4] {'fsdp_0','fsdp_1'}, dimensions={0} | all-to-all | bytes 5242880 | tf_op jit(solution)/shard_map/all_to_all | solution.py:34
  189.5 1.9 reduce_sum.36
  194.6 10.5 %psum.28 = f32[]{:T(128)} all-reduce(f32[]{:T(128)S(6)} %add.70), channel_id=1, replica_groups=mesh['dp_0'=4,'dp_1'=2,'fsdp_0'=4,'fsdp_1'=4] {'dp_0'}, use_global_device_ids=true, to_apply=%region_6.0 | all-reduce | flops 1 | bytes 8 | tf_op jit(solution)/shard_map/psum | solution.py:49
  205.1 3.1 %psum.29 = f32[]{:T(128)} all-reduce(f32[]{:T(128)} %psum.28), channel_id=1, replica_groups=mesh['dp_0'=4,'dp_1'=2,'fsdp_0'=4,'fsdp_1'=4] {'dp_1'}, use_global_device_ids=true, to_apply=%region_7.0 | all-reduce | flops 1 | bytes 8 | tf_op jit(solution)/shard_map/psum | solution.py:49
  208.2 9.2 %psum.30 = f32[]{:T(128)} all-reduce(f32[]{:T(128)} %psum.29), channel_id=1, replica_groups=mesh['dp_0'=4,'dp_1'=2,'fsdp_0'=4,'fsdp_1'=4] {'fsdp_0'}, use_global_device_ids=true, to_apply=%region_8.0 | all-reduce | flops 1 | bytes 8 | tf_op jit(solution)/shard_map/psum | solution.py:49
  217.4 9.7 %psum.31 = f32[]{:T(128)} all-reduce(f32[]{:T(128)} %psum.30), channel_id=1, replica_groups=mesh['dp_0'=4,'dp_1'=2,'fsdp_0'=4,'fsdp_1'=4] {'fsdp_1'}, use_global_device_ids=true, to_apply=%region_9.0 | all-reduce | flops 1 | bytes 8 | tf_op jit(solution)/shard_map/psum | solution.py:49
  229.2 1.2 broadcast_in_dim.2
  230.4 3.7 %all-to-all-start.1 = ((bf16[16,32,1280]{2,1,0:T(8,128)(2,1)}), bf16[16,32,1280]{2,1,0:T(8,128)(2,1)S(1)}, u32[]{:S(2)}, u32[]{:S(2)}) async-start(bf16[16,32,1280]{2,1,0:T(8,128)(2,1)} %broadcast_in_dim.2), calls=%async_computation.3 | async-start | bytes 2621440 | tf_op jit(solution)/shard_map/all_to_all | solution.py:55
  234.1 1.3 copy.27
  235.5 2.4 copy.28
  239.0 12.6 %all-to-all-done.1 = bf16[16,32,1280]{2,1,0:T(8,128)(2,1)S(1)} async-done(((bf16[16,32,1280]{2,1,0:T(8,128)(2,1)}), bf16[16,32,1280]{2,1,0:T(8,128)(2,1)S(1)}, u32[]{:S(2)}, u32[]{:S(2)}) %all-to-all-start.1) | async-done | bytes 1310752 | tf_op jit(solution)/shard_map/all_to_all | solution.py:55
  251.6 1.1 copy-done.1
  252.7 2.9 %fusion.2 = f32[512,1024]{0,1:T(8,128)S(1)} fusion(bf16[512,1024]{0,1:T(8,128)(2,1)} %copy.28, bf16[512,1024]{0,1:T(8,128)(2,1)} %copy.27, bf16[512,512]{1,0:T(8,128)(2,1)} %param.21, bf16[512,1280]{1,0:T(8,128)(2,1)} %bitcast.34), kind=kOutput, calls=%fused_computation.5 | convolution fusion | flops 539492352 | bytes 5767168 | tf_op jit(solution)/shard_map/dot_general | solution.py:140
  255.6 1.8 copy.33
  257.4 1.4 fusion.8
  259.6 1.4 fusion.7
  (46 shorter events, 7.3 us)
Async XLA Ops:
  7.2 1.2 copy-start
  7.2 3.0 %copy-start.4 = (bf16[1,512,1024]{2,1,0:T(8,128)(2,1)S(1)}, bf16[1,512,1024]{2,1,0:T(8,128)(2,1)}, u32[]{:S(2)}) copy-start(bf16[1,512,1024]{2,1,0:T(8,128)(2,1)} %param.19) | copy-start | bytes 3145732
  7.2 3.0 %copy-start.3 = (bf16[512,512]{1,0:T(8,128)(2,1)S(1)}, bf16[512,512]{1,0:T(8,128)(2,1)}, u32[]{:S(2)}) copy-start(bf16[512,512]{1,0:T(8,128)(2,1)} %param.22) | copy-start | bytes 1572868
  7.2 46.8 %reduce-scatter.5.cloned.1.call-start = ((), (), s32[]{:S(2)}) async-start(), calls=%async_computation.5 | async-start | bytes 4718592 | tf_op jit(solution)/shard_map/reduce_scatter | solution.py:19
  13.4 1.0 copy-start.2
  13.4 133.8 %reduce-scatter.3.cloned.1.call-start = ((), (), s32[]{:S(2)}) async-start(), calls=%async_computation.4 | async-start | bytes 18874368 | tf_op jit(solution)/shard_map/reduce_scatter | solution.py:118
  189.4 38.3 %copy-start.6 = (f32[32,1024]{1,0:T(8,128)S(1)}, f32[32,1024]{1,0:T(8,128)}, u32[]{:S(2)}) copy-start(f32[32,1024]{1,0:T(8,128)} %param.30) | copy-start | bytes 393220
  189.4 38.3 %copy-start.7 = (f32[32,1024]{1,0:T(8,128)S(1)}, f32[32,1024]{1,0:T(8,128)}, u32[]{:S(2)}) copy-start(f32[32,1024]{1,0:T(8,128)} %param.33) | copy-start | bytes 393220
  189.4 39.1 %copy-start.12 = (f32[32,128]{1,0:T(8,128)S(1)}, f32[32,128]{1,0:T(8,128)}, u32[]{:S(2)}) copy-start(f32[32,128]{1,0:T(8,128)} %param.31) | copy-start | bytes 49156
  189.5 39.1 %copy-start.13 = (f32[32,128]{1,0:T(8,128)S(1)}, f32[32,128]{1,0:T(8,128)}, u32[]{:S(2)}) copy-start(f32[32,128]{1,0:T(8,128)} %param.34) | copy-start | bytes 49156
  189.5 39.1 %copy-start.14 = (f32[32,128]{1,0:T(8,128)S(1)}, f32[32,128]{1,0:T(8,128)}, u32[]{:S(2)}) copy-start(f32[32,128]{1,0:T(8,128)} %param.35) | copy-start | bytes 49156
  189.5 39.1 %copy-start.15 = (f32[32,128]{1,0:T(8,128)S(1)}, f32[32,128]{1,0:T(8,128)}, u32[]{:S(2)}) copy-start(f32[32,128]{1,0:T(8,128)} %param.32) | copy-start | bytes 49156
  229.2 4.9 %copy-start.5 = (bf16[512,1024]{1,0:T(8,128)(2,1)S(1)}, bf16[512,1024]{1,0:T(8,128)(2,1)}, u32[]{:S(2)}) copy-start(bf16[512,1024]{1,0:T(8,128)(2,1)} %param.24) | copy-start | bytes 3145732
  230.4 21.2 %all-to-all-start.1 = ((bf16[16,32,1280]{2,1,0:T(8,128)(2,1)}), bf16[16,32,1280]{2,1,0:T(8,128)(2,1)S(1)}, u32[]{:S(2)}, u32[]{:S(2)}) async-start(bf16[16,32,1280]{2,1,0:T(8,128)(2,1)} %broadcast_in_dim.2), calls=%async_computation.3 | async-start | bytes 2621440 | tf_op jit(solution)/shard_map/all_to_all | solution.py:55
  235.5 2.4 copy-start.8
  235.5 2.5 copy-start.9
  235.5 3.3 %copy-start.10 = (bf16[512,128]{1,0:T(8,128)(2,1)S(1)}, bf16[512,128]{1,0:T(8,128)(2,1)}, u32[]{:S(2)}) copy-start(bf16[512,128]{1,0:T(8,128)(2,1)} %param.26) | copy-start | bytes 393220
  235.5 3.4 %copy-start.11 = (bf16[512,128]{1,0:T(8,128)(2,1)S(1)}, bf16[512,128]{1,0:T(8,128)(2,1)}, u32[]{:S(2)}) copy-start(bf16[512,128]{1,0:T(8,128)(2,1)} %param.29) | copy-start | bytes 393220
  251.6 1.1 copy-start.1
Sparse Core Ops, SparseCore 0:
  13.5 40.4 reduce-scatter.4
  56.5 90.6 reduce-scatter.2
where the time goes:
time: 269 us
  waiting for transfers between devices  133 us (49%)
  blocking collectives  72.9 us (27%)
  matrix products  20 us (7%)
  between operations  16.9 us (6%)
  local copies, waits for them, and re-layouts  13.8 us (5%)
  other arithmetic  8.86 us (3%)
  starting transfers between devices  3.78 us (1%)
    reduce_scatter x1, waiting for transfers between devices, shards(): lax.psum_scatter(complete[0], DP, scatter_dimension=1, tiled=True)  92.1 us
    all_to_all x1, blocking collectives, sum_at_owner(): lax.all_to_all(pieces, axis, split_axis=0, concat_axis=0, tiled=True)  40.4 us
    psum x4, blocking collectives, over_axes(): x = lax.psum(x, axis)  32.5 us
    reduce_scatter x1, waiting for transfers between devices, in_one_piece(): lax.psum_scatter(both, axis, scatter_dimension=dim, tiled=True)  27.8 us
    dot_general x3, matrix products, shards(): lax.dot_general(projector, gradient, contract_rows, preferred_element_typ...  14.2 us
    all_to_all x1, waiting for transfers between devices, from_everyone(): lax.all_to_all(jnp.broadcast_to(x[None], (devices, *x.shape)), axis, 0, 0...  12.6 us
    unnamed x41, local copies, waits for them, and re-layouts  11.5 us
    dot_general x3, matrix products, shards(): jnp.dot(projector, piece, preferred_element_type=jnp.float32)  5.74 us
  transfers between devices with their start and end apart: 3, of which 3 were waited for; matrix products, arithmetic and copies ran while one was open for 7% of the time, Pallas kernels for 0%

commit v1 on v0

--- a/solution.py
+++ b/solution.py
@@ -46,7 +46,7 @@
 
 def over_axes(x, axes):
     for axis in axes:
-        x = lax.psum(x, axis)
+        x = jnp.sum(lax.all_gather(x, axis_name=axis), 0)
     return x
 
 

time: 269 us -> 285 us (1.059)
  blocking collectives: 72.9 us -> 32.5 us
  waiting for transfers between devices: 133 us -> 170 us
  local copies, waits for them, and re-layouts: 13.8 us -> 21.1 us
  starting transfers between devices: 3.78 us -> 10.9 us
  other arithmetic: 8.86 us -> 12.7 us
    all_to_all x1 -> x0, blocking collectives: 40.4 us -> none  [sum_at_owner(): lax.all_to_all(pieces, axis, split_axis=0, concat_axis=0, tiled=True)]
    all_to_all x0 -> x1, waiting for transfers between devices: none -> 37.4 us  [sum_at_owner(): lax.all_to_all(pieces, axis, split_axis=0, concat_axis=0, tiled=True)]
    unnamed x0 -> x4, blocking collectives: none -> 32.5 us
    psum x4 -> x0, blocking collectives: 32.5 us -> none  [over_axes(): x = lax.psum(x, axis)]
    unnamed x41 -> x61, local copies, waits for them, and re-layouts: 11.5 us -> 18.9 us
    all_to_all x0 -> x1, starting transfers between devices: none -> 7.11 us  [sum_at_owner(): lax.all_to_all(pieces, axis, split_axis=0, concat_axis=0, tiled=True)]
  transfers between devices with their start and end apart: 3 -> 4, of which waited for: 3 -> 4; matrix products, arithmetic and copies ran while one was open for 7% -> 6% of each run, Pallas kernels for 0% -> 0%
where the time goes in v1:
time: 285 us; the launch traced here: 284 us
  waiting for transfers between devices  170 us (60%)
  blocking collectives  32.5 us (11%)
  local copies, waits for them, and re-layouts  21.1 us (7%)
  matrix products  20 us (7%)
  between operations  17 us (6%)
  other arithmetic  12.7 us (4%)
  starting transfers between devices  10.9 us (4%)
    reduce_scatter x1, waiting for transfers between devices, shards(): lax.psum_scatter(complete[0], DP, scatter_dimension=1, tiled=True)  92.1 us
    all_to_all x1, waiting for transfers between devices, sum_at_owner(): lax.all_to_all(pieces, axis, split_axis=0, concat_axis=0, tiled=True)  37.4 us
    unnamed x4, blocking collectives  32.5 us
    reduce_scatter x1, waiting for transfers between devices, in_one_piece(): lax.psum_scatter(both, axis, scatter_dimension=dim, tiled=True)  27.8 us
    unnamed x61, local copies, waits for them, and re-layouts  18.9 us
    dot_general x3, matrix products, shards(): lax.dot_general(projector, gradient, contract_rows, preferred_element_typ...  14.2 us
    all_to_all x1, waiting for transfers between devices, from_everyone(): lax.all_to_all(jnp.broadcast_to(x[None], (devices, *x.shape)), axis, 0, 0...  12.6 us
    all_to_all x1, starting transfers between devices, sum_at_owner(): lax.all_to_all(pieces, axis, split_axis=0, concat_axis=0, tiled=True)  7.11 us
  transfers between devices with their start and end apart: 4, of which 4 were waited for; matrix products, arithmetic and copies ran while one was open for 6% of the time, Pallas kernels for 0%

profile of v1, /device:TPU:0, one launch (start us, length us, event | category | flops | bytes accessed | tf_op | source)
XLA Modules:
  0.0 284.2 jit_solution(11848032724694421629)
XLA Ops:
  8.4 1.8 fusion.10
  10.9 2.5 pad_maximum_fusion
  14.4 11.7 %fusion = f32[512,8192]{1,0:T(8,128)} fusion(bf16[512,512]{1,0:T(8,128)(2,1)S(1)} %copy-done.2, bf16[1,512,8192]{2,1,0:T(8,128)(2,1)} %param.18), kind=kOutput, calls=%fused_computation | convolution fusion | flops 4294967296 | bytes 25690112 | tf_op jit(solution)/shard_map/dot_general | solution.py:114
  26.2 27.8 %reduce-scatter.5.cloned.1.call-done = f32[1024,128]{1,0:T(8,128)} async-done(((f32[1024,1024]{1,0:T(8,128)}), f32[1024,128]{1,0:T(8,128)}) %reduce-scatter.5.cloned.1.call-update) | async-done | bytes 524304 | tf_op jit(solution)/shard_map/reduce_scatter | solution.py:19
  55.1 92.1 %reduce-scatter.3.cloned.1.call-done = f32[512,1024]{1,0:T(8,128)} async-done(((f32[512,8192]{1,0:T(8,128)}), f32[512,1024]{1,0:T(8,128)}) %reduce-scatter.3.cloned.1.call-update) | async-done | bytes 2097168 | tf_op jit(solution)/shard_map/reduce_scatter | solution.py:118
  147.2 3.3 %pad_maximum_fusion.1 = f32[512,1280]{1,0:T(8,128)} fusion(f32[512,128]{1,0:T(8,128)S(1)} %get-tuple-element.30, f32[512,128]{1,0:T(8,128)S(1)} %get-tuple-element.29, f32[512,1024]{1,0:T(8,128)} %reduce-scatter.3.cloned.1.call-done), kind=kLoop, calls=%fused_computation.3 | loop fusion | flops 1310720 | bytes 5242880 | tf_op jit(solution)/shard_map/concatenate | solution.py:43
  150.5 7.1 %all-to-all-start = ((f32[16,32,1280]{2,1,0:T(8,128)}), f32[16,32,1280]{2,1,0:T(8,128)}, u32[]{:S(2)}, u32[]{:S(2)}) async-start(f32[16,32,1280]{2,1,0:T(8,128)} %bitcast.41), calls=%async_computation.2 | async-start | bytes 5242880 | tf_op jit(solution)/shard_map/all_to_all | solution.py:34
  158.4 37.4 %all-to-all-done = f32[16,32,1280]{2,1,0:T(8,128)} async-done(((f32[16,32,1280]{2,1,0:T(8,128)}), f32[16,32,1280]{2,1,0:T(8,128)}, u32[]{:S(2)}, u32[]{:S(2)}) %all-to-all-start) | async-done | bytes 2621472 | tf_op jit(solution)/shard_map/all_to_all | solution.py:34
  195.8 1.9 reduce_sum.72
  202.2 12.1 %all-reduce = f32[4]{0:T(128)S(1)} all-reduce(f32[4]{0:T(128)S(1)} %dynamic-update-slice), channel_id=1, replica_groups=mesh['dp_0'=4,'dp_1'=2,'fsdp_0'=4,'fsdp_1'=4] {'dp_0'}, use_global_device_ids=true, to_apply=%add | all-reduce | flops 4 | bytes 32
  214.9 1.4 dynamic-update-slice.1
  216.9 2.4 all-reduce.1
  219.9 1.4 dynamic-update-slice.2
  221.9 9.3 %all-reduce.2 = f32[4]{0:T(128)S(1)} all-reduce(f32[4]{0:T(128)S(1)} %dynamic-update-slice.2), channel_id=1, replica_groups=mesh['dp_0'=4,'dp_1'=2,'fsdp_0'=4,'fsdp_1'=4] {'fsdp_0'}, use_global_device_ids=true, to_apply=%add.2 | all-reduce | flops 4 | bytes 32
  231.8 1.4 dynamic-update-slice.3
  233.2 8.7 %all-reduce.3 = f32[4]{0:T(128)S(1)} all-reduce(f32[4]{0:T(128)S(1)} %dynamic-update-slice.3), channel_id=1, replica_groups=mesh['dp_0'=4,'dp_1'=2,'fsdp_0'=4,'fsdp_1'=4] {'fsdp_1'}, use_global_device_ids=true, to_apply=%add.3 | all-reduce | flops 4 | bytes 32
  245.9 3.7 %all-to-all-start.1 = ((bf16[16,32,1280]{2,1,0:T(8,128)(2,1)}), bf16[16,32,1280]{2,1,0:T(8,128)(2,1)S(1)}, u32[]{:S(2)}, u32[]{:S(2)}) async-start(bf16[16,32,1280]{2,1,0:T(8,128)(2,1)} %broadcast_in_dim.2), calls=%async_computation.3 | async-start | bytes 2621440 | tf_op jit(solution)/shard_map/all_to_all | solution.py:55
  249.6 1.3 copy.27
  250.9 2.4 copy.28
  254.4 12.6 %all-to-all-done.1 = bf16[16,32,1280]{2,1,0:T(8,128)(2,1)S(1)} async-done(((bf16[16,32,1280]{2,1,0:T(8,128)(2,1)}), bf16[16,32,1280]{2,1,0:T(8,128)(2,1)S(1)}, u32[]{:S(2)}, u32[]{:S(2)}) %all-to-all-start.1) | async-done | bytes 1310752 | tf_op jit(solution)/shard_map/all_to_all | solution.py:55
  268.1 2.9 %fusion.2 = f32[512,1024]{0,1:T(8,128)S(1)} fusion(bf16[512,1024]{0,1:T(8,128)(2,1)} %copy.28, bf16[512,1024]{0,1:T(8,128)(2,1)} %copy.27, bf16[512,512]{1,0:T(8,128)(2,1)} %param.21, bf16[512,1280]{1,0:T(8,128)(2,1)} %bitcast.42), kind=kOutput, calls=%fused_computation.5 | convolution fusion | flops 539492352 | bytes 5767168 | tf_op jit(solution)/shard_map/dot_general | solution.py:140
  271.0 1.8 copy.33
  272.8 1.4 fusion.8
  275.1 1.4 fusion.7
  (71 shorter events, 17.3 us)
Async XLA Ops:
  7.2 1.2 copy-start
  7.2 3.0 %copy-start.4 = (bf16[1,512,1024]{2,1,0:T(8,128)(2,1)S(1)}, bf16[1,512,1024]{2,1,0:T(8,128)(2,1)}, u32[]{:S(2)}) copy-start(bf16[1,512,1024]{2,1,0:T(8,128)(2,1)} %param.19) | copy-start | bytes 3145732
  7.2 3.0 %copy-start.3 = (bf16[512,512]{1,0:T(8,128)(2,1)S(1)}, bf16[512,512]{1,0:T(8,128)(2,1)}, u32[]{:S(2)}) copy-start(bf16[512,512]{1,0:T(8,128)(2,1)} %param.22) | copy-start | bytes 1572868
  7.2 46.8 %reduce-scatter.5.cloned.1.call-start = ((), (), s32[]{:S(2)}) async-start(), calls=%async_computation.5 | async-start | bytes 4718592 | tf_op jit(solution)/shard_map/reduce_scatter | solution.py:19
  13.4 1.0 copy-start.2
  13.4 133.8 %reduce-scatter.3.cloned.1.call-start = ((), (), s32[]{:S(2)}) async-start(), calls=%async_computation.4 | async-start | bytes 18874368 | tf_op jit(solution)/shard_map/reduce_scatter | solution.py:118
  150.5 7.2 %copy-start.19 = (u32[128]{0:T(128)S(1)}, u32[128]{0:T(128)}, u32[]{:S(2)}) copy-start(u32[128]{0:T(128)} %constant.43) | copy-start | bytes 1540
  150.5 45.2 %all-to-all-start = ((f32[16,32,1280]{2,1,0:T(8,128)}), f32[16,32,1280]{2,1,0:T(8,128)}, u32[]{:S(2)}, u32[]{:S(2)}) async-start(f32[16,32,1280]{2,1,0:T(8,128)} %bitcast.41), calls=%async_computation.2 | async-start | bytes 5242880 | tf_op jit(solution)/shard_map/all_to_all | solution.py:34
  157.7 43.9 %copy-start.18 = (u32[128]{0:T(128)S(1)}, u32[128]{0:T(128)}, u32[]{:S(2)}) copy-start(u32[128]{0:T(128)} %constant.48) | copy-start | bytes 1540
  157.7 58.6 %copy-start.17 = (u32[128]{0:T(128)S(1)}, u32[128]{0:T(128)}, u32[]{:S(2)}) copy-start(u32[128]{0:T(128)} %constant.53) | copy-start | bytes 1540
  157.7 63.6 %copy-start.16 = (u32[128]{0:T(128)S(1)}, u32[128]{0:T(128)}, u32[]{:S(2)}) copy-start(u32[128]{0:T(128)} %constant.58) | copy-start | bytes 1540
  157.7 85.5 %copy-start.6 = (f32[32,1024]{1,0:T(8,128)S(1)}, f32[32,1024]{1,0:T(8,128)}, u32[]{:S(2)}) copy-start(f32[32,1024]{1,0:T(8,128)} %param.30) | copy-start | bytes 393220
  157.7 85.5 %copy-start.7 = (f32[32,1024]{1,0:T(8,128)S(1)}, f32[32,1024]{1,0:T(8,128)}, u32[]{:S(2)}) copy-start(f32[32,1024]{1,0:T(8,128)} %param.33) | copy-start | bytes 393220
  157.7 86.3 %copy-start.12 = (f32[32,128]{1,0:T(8,128)S(1)}, f32[32,128]{1,0:T(8,128)}, u32[]{:S(2)}) copy-start(f32[32,128]{1,0:T(8,128)} %param.31) | copy-start | bytes 49156
  157.7 86.3 %copy-start.13 = (f32[32,128]{1,0:T(8,128)S(1)}, f32[32,128]{1,0:T(8,128)}, u32[]{:S(2)}) copy-start(f32[32,128]{1,0:T(8,128)} %param.34) | copy-start | bytes 49156
  157.7 86.3 %copy-start.14 = (f32[32,128]{1,0:T(8,128)S(1)}, f32[32,128]{1,0:T(8,128)}, u32[]{:S(2)}) copy-start(f32[32,128]{1,0:T(8,128)} %param.35) | copy-start | bytes 49156
  157.8 86.3 %copy-start.15 = (f32[32,128]{1,0:T(8,128)S(1)}, f32[32,128]{1,0:T(8,128)}, u32[]{:S(2)}) copy-start(f32[32,128]{1,0:T(8,128)} %param.32) | copy-start | bytes 49156
  244.7 4.9 %copy-start.5 = (bf16[512,1024]{1,0:T(8,128)(2,1)S(1)}, bf16[512,1024]{1,0:T(8,128)(2,1)}, u32[]{:S(2)}) copy-start(bf16[512,1024]{1,0:T(8,128)(2,1)} %param.24) | copy-start | bytes 3145732
  245.9 21.2 %all-to-all-start.1 = ((bf16[16,32,1280]{2,1,0:T(8,128)(2,1)}), bf16[16,32,1280]{2,1,0:T(8,128)(2,1)S(1)}, u32[]{:S(2)}, u32[]{:S(2)}) async-start(bf16[16,32,1280]{2,1,0:T(8,128)(2,1)} %broadcast_in_dim.2), calls=%async_computation.3 | async-start | bytes 2621440 | tf_op jit(solution)/shard_map/all_to_all | solution.py:55
  250.9 2.4 copy-start.8
  250.9 2.5 copy-start.9
  250.9 3.3 %copy-start.10 = (bf16[512,128]{1,0:T(8,128)(2,1)S(1)}, bf16[512,128]{1,0:T(8,128)(2,1)}, u32[]{:S(2)}) copy-start(bf16[512,128]{1,0:T(8,128)(2,1)} %param.26) | copy-start | bytes 393220
  250.9 3.4 %copy-start.11 = (bf16[512,128]{1,0:T(8,128)(2,1)S(1)}, bf16[512,128]{1,0:T(8,128)(2,1)}, u32[]{:S(2)}) copy-start(bf16[512,128]{1,0:T(8,128)(2,1)} %param.29) | copy-start | bytes 393220
  267.0 1.1 copy-start.1
Sparse Core Ops, SparseCore 0:
  13.5 40.4 reduce-scatter.4
  56.5 90.6 reduce-scatter.2
